TPU v7x, 128 devices: a whole 4x4x4 slice. The times are simulated.
128 devices in a mesh: row: 16 (over y, z), col: 8 (over x, core).
Axes of the slice: x: 4, y: 4, z: 4, core: 2. Of those that a mesh axis runs over, the one named last changes fastest.
Arguments:
- grid_values: bfloat16 [512, 256, 384], P(('row', 'col')), may hold values from -0.109375 to 0.109375
- external: float32 [512, 256], P(('row', 'col')), may hold values from 0 to 6
- tiles: int32 [512, 3], P(('row', 'col')), may hold values from 0 to 15, as said below
- kinetic: bfloat16 [16384, 16384], P('row', 'col'), may hold values from -0.046875 to 0.046875
- orbitals: bfloat16 [16384, 256], P(('row', 'col')), may hold values from -6 to 6
Outputs:
- filtered: float32 [16384, 256], P(('row', 'col'))
Inputs may be any that keep to these rules, and one draw needn't show every extreme that they name: Each batch names 3 distinct tiles in increasing order. Among the 4 batches of one device no tile is named more than 2 times; in every draw some tile is named exactly 2 times by the batches of every device.
All inputs are finite; a program needn't handle non-finite values.
Results may differ from a plain program's by a relative error of at most 0.0064.
Values may be sent and summed in bfloat16 or wider, within the bound.
A program may use at most 128 MiB of HBM per device.

v0:
```python
import jax
import jax.numpy as jnp
from jax import lax
from jax.sharding import PartitionSpec as P

TILE = 128
LISTED = 3
LIST = 384


center = 1.0
spread = 2.5


def body(grid_values, external, tiles, kinetic, orbitals):
    row_count = lax.axis_size("row")
    shard_rows, orbital_count = orbitals.shape
    per_shard = shard_rows // TILE
    group_tiles = row_count * per_shard
    batch_count = tiles.shape[0]
    group_orbitals = lax.all_gather(orbitals, "row", axis=0, tiled=True)
    listed_orbitals = group_orbitals.reshape(group_tiles, TILE, orbital_count)[tiles].reshape(
        batch_count, LIST, orbital_count
    )
    waves = jnp.einsum(
        "bpl,blk->bpk", grid_values, listed_orbitals, preferred_element_type=jnp.float32
    )
    density = jnp.sum(waves * waves, axis=2)
    potential = external - jnp.cbrt(3.0 * density / jnp.pi)
    weighted = (potential[:, :, None] * grid_values).astype(jnp.bfloat16)
    integrals = jnp.einsum(
        "bpl,bpm->blm", grid_values, weighted, preferred_element_type=jnp.float32
    )
    blocks = integrals.reshape(batch_count, LISTED, TILE, LISTED, TILE).transpose(0, 1, 3, 2, 4)
    dense_local = (
        jnp.zeros((group_tiles, TILE, group_tiles, TILE), jnp.float32)
        .at[tiles[:, :, None], :, tiles[:, None, :], :]
        .add(blocks)
    )
    dense_local = dense_local.reshape(group_tiles * TILE, group_tiles * TILE)
    grid_rows = lax.psum_scatter(dense_local, "row", scatter_dimension=0, tiled=True)
    row_start = lax.axis_index("col") * shard_rows
    updated = (
        lax.dynamic_slice_in_dim(kinetic, row_start, shard_rows, 0).astype(jnp.float32) + grid_rows
    )
    hamiltonian = lax.dynamic_update_slice_in_dim(
        kinetic, updated.astype(jnp.bfloat16), row_start, 0
    )

    def add_piece(piece):
        return jnp.dot(hamiltonian, piece, preferred_element_type=jnp.float32)

    def times_ham(vectors):
        return add_piece(lax.all_gather(vectors, "row", axis=0, tiled=True))

    def filter_step(partial_value, vectors):
        reduced = lax.psum_scatter(partial_value, "col", scatter_dimension=0, tiled=True)
        return reduced / spread - center / spread * vectors.astype(jnp.float32)

    first_term = filter_step(
        jnp.dot(hamiltonian, group_orbitals, preferred_element_type=jnp.float32), orbitals
    ).astype(jnp.bfloat16)
    second_term = (
        2.0 * filter_step(times_ham(first_term), first_term) - orbitals.astype(jnp.float32)
    ).astype(jnp.bfloat16)
    return 2.0 * filter_step(times_ham(second_term), second_term) - first_term.astype(jnp.float32)


def solution(mesh):
    return jax.shard_map(
        body,
        mesh=mesh,
        in_specs=(
            P(("row", "col"), None, None),
            P(("row", "col"), None),
            P(("row", "col"), None),
            P("row", "col"),
            P(("row", "col"), None),
        ),
        out_specs=P(("row", "col"), None),
        check_vma=False,
    )
```

profile of v0, /device:TPU:0, one launch (start us, length us, event | category | flops | bytes accessed | tf_op | source)
XLA Modules:
  0.0 428.9 jit_solution(10878357735825306583)
XLA Ops:
  6.5 0.0 copy-start.5
  6.5 0.0 copy-start
  6.5 0.0 copy-start.6
  6.5 0.0 all-gather.4.cloned.1.call-start
  6.5 4.8 %copy.28 = bf16[1024,2048]{1,0:T(8,128)(2,1)} copy(bf16[1024,2048]{1,0:T(8,128)(2,1)} %param.8) | data formatting | bytes 8388608
  11.3 0.0 all-gather.4.cloned.1.call-update
  11.4 0.0 reduce-scatter.5.cloned.1.call-start
  11.4 0.0 copy-done.5
  11.5 0.1 or_select_fusion
  11.5 0.1 reshape.38
  11.6 0.1 reshape.32
  11.7 44.9 %all-gather.4.cloned.1.call-done = bf16[2048,256]{1,0:T(8,128)(2,1)} async-done(((bf16[128,256]{1,0:T(8,128)(2,1)}), bf16[2048,256]{1,0:T(8,128)(2,1)}) %all-gather.4.cloned.1.call-update) | async-done | bytes 1048592 | tf_op jit(solution)/shard_map/all_gather | solution.py:21
  56.7 1.8 gather_fusion
  58.5 0.0 copy-done
  58.5 0.5 fusion
  59.0 0.0 copy-done.6
  59.0 0.9 convolution_bitcast_fusion
  60.0 2.0 copy.17
  62.0 4.5 %reshape.28 = f32[4,3,128,3,128]{4,3,2,1,0:T(4,128)} reshape(f32[4,384,384]{2,1,0:T(8,128)} %copy.17) | data formatting | bytes 4718592 | tf_op jit(solution)/shard_map/reshape | solution.py:34
  66.5 2.2 copy.18
  68.7 7.9 %broadcast_in_dim.8 = f32[16,128,16,128]{3,1,2,0:T(8,128)} broadcast(f32[]{:T(128)} %constant.13.clone.1), dimensions={} | broadcast | bytes 16777220 | tf_op jit(solution)/shard_map/broadcast_in_dim | solution.py:36
  76.6 9.1 %scatter_fusion = f32[16,128,16,128]{3,1,2,0:T(8,128)} fusion(f32[16,128,16,128]{3,1,2,0:T(8,128)} %broadcast_in_dim.8, s32[36]{0:T(128)S(1)} %reshape.38, f32[36,128,128]{2,1,0:T(8,128)S(1)} %bitcast.24), kind=kCustom, calls=%fused_computation.1 | custom fusion | flops 589824 | bytes 7078176 | tf_op jit(solution)/shard_map/scatter-add | solution.py:38
  85.7 15.5 %copy.19 = f32[16,128,16,128]{3,2,1,0:T(8,128)S(1)} copy(f32[16,128,16,128]{3,1,2,0:T(8,128)} %scatter_fusion) | data formatting | bytes 33554432 | tf_op jit(solution)/shard_map/scatter-add | solution.py:38
  101.2 11.2 %copy.24 = f32[256,8,16,128]{3,1,2,0:T(8,128)} copy(f32[256,8,16,128]{3,2,1,0:T(8,128)S(1)} %bitcast.23) | data formatting | bytes 33554432
  112.3 0.0 copy-start.2
  112.3 0.0 reduce-scatter.5.cloned.1.call-update
  112.4 0.2 reduce-scatter.7.cloned.1.call-start
  112.6 110.1 %reduce-scatter.5.cloned.1.call-done = f32[128,2048]{1,0:T(8,128)} async-done(((f32[2048,2048]{1,0:T(8,128)}), f32[128,2048]{1,0:T(8,128)}) %reduce-scatter.5.cloned.1.call-update) | async-done | bytes 1048592 | tf_op jit(solution)/shard_map/reduce_scatter | solution.py:41
  222.7 2.3 fusion.2
  225.0 0.0 copy-done.2
  225.0 0.0 copy-start.3
  225.0 4.4 %fusion.8 = f32[1024,256]{1,0:T(8,128)} fusion(bf16[1024,2048]{1,0:T(8,128)(2,1)} %fusion.2, bf16[2048,256]{1,0:T(8,128)(2,1)S(1)} %copy-done.2), kind=kOutput, calls=%fused_computation.26 | convolution fusion | flops 1073741824 | bytes 6291456 | tf_op jit(solution)/shard_map/dot_general | solution.py:61
  229.5 0.0 reduce-scatter.7.cloned.1.call-update
  229.5 0.0 all-gather.6.cloned.1.call-start
  229.5 31.4 %reduce-scatter.7.cloned.1.call-done = f32[128,256]{1,0:T(8,128)} async-done(((f32[1024,256]{1,0:T(8,128)}), f32[128,256]{1,0:T(8,128)}) %reduce-scatter.7.cloned.1.call-update) | async-done | bytes 131088 | tf_op jit(solution)/shard_map/reduce_scatter | solution.py:57
  261.0 0.0 copy-done.3
  261.0 1.6 fusion.4
  262.5 0.0 all-gather.6.cloned.1.call-update
  262.6 0.0 copy-start.1
  262.6 0.0 reduce-scatter.9.cloned.1.call-start
  262.6 41.8 %all-gather.6.cloned.1.call-done = bf16[2048,256]{1,0:T(8,128)(2,1)} async-done(((bf16[128,256]{1,0:T(8,128)(2,1)}), bf16[2048,256]{1,0:T(8,128)(2,1)}) %all-gather.6.cloned.1.call-update) | async-done | bytes 1048592 | tf_op jit(solution)/shard_map/all_gather | solution.py:54
  304.4 4.7 %fusion.9 = f32[1024,256]{1,0:T(8,128)} fusion(bf16[1024,2048]{1,0:T(8,128)(2,1)} %fusion.2, bf16[2048,256]{1,0:T(8,128)(2,1)} %all-gather.6.cloned.1.call-done), kind=kOutput, calls=%fused_computation.27 | convolution fusion | flops 1073741824 | bytes 6291456 | tf_op jit(solution)/shard_map/dot_general | solution.py:51
  309.1 0.0 reduce-scatter.9.cloned.1.call-update
  309.2 0.0 all-gather.8.cloned.1.call-start
  309.2 31.5 %reduce-scatter.9.cloned.1.call-done = f32[128,256]{1,0:T(8,128)} async-done(((f32[1024,256]{1,0:T(8,128)}), f32[128,256]{1,0:T(8,128)}) %reduce-scatter.9.cloned.1.call-update) | async-done | bytes 131088 | tf_op jit(solution)/shard_map/reduce_scatter | solution.py:57
  340.7 0.0 copy-done.1
  340.7 1.6 fusion.5
  342.3 0.0 all-gather.8.cloned.1.call-update
  342.3 0.0 copy-start.4
  342.3 0.0 reduce-scatter.11.cloned.1.call-start
  342.3 41.9 %all-gather.8.cloned.1.call-done = bf16[2048,256]{1,0:T(8,128)(2,1)} async-done(((bf16[128,256]{1,0:T(8,128)(2,1)}), bf16[2048,256]{1,0:T(8,128)(2,1)}) %all-gather.8.cloned.1.call-update) | async-done | bytes 1048592 | tf_op jit(solution)/shard_map/all_gather | solution.py:54
  384.2 4.7 %fusion.10 = f32[1024,256]{1,0:T(8,128)} fusion(bf16[1024,2048]{1,0:T(8,128)(2,1)} %fusion.2, bf16[2048,256]{1,0:T(8,128)(2,1)} %all-gather.8.cloned.1.call-done), kind=kOutput, calls=%fused_computation.28 | convolution fusion | flops 1073741824 | bytes 6291456 | tf_op jit(solution)/shard_map/dot_general | solution.py:51
  388.9 0.0 reduce-scatter.11.cloned.1.call-update
  389.0 31.5 %reduce-scatter.11.cloned.1.call-done = f32[128,256]{1,0:T(8,128)} async-done(((f32[1024,256]{1,0:T(8,128)}), f32[128,256]{1,0:T(8,128)}) %reduce-scatter.11.cloned.1.call-update) | async-done | bytes 131088 | tf_op jit(solution)/shard_map/reduce_scatter | solution.py:57
  420.5 0.0 copy-done.4
  420.5 1.6 convert_subtract_fusion
  (4 shorter events, 0.0 us)
Async XLA Ops:
  6.5 4.9 %copy-start.5 = (s32[4,3]{1,0:T(4,128)S(1)}, s32[4,3]{1,0:T(4,128)}, u32[]{:S(2)}) copy-start(s32[4,3]{1,0:T(4,128)} %param.7) | copy-start | bytes 148
  6.5 52.0 %copy-start = (bf16[4,256,384]{2,1,0:T(8,128)(2,1)S(1)}, bf16[4,256,384]{2,1,0:T(8,128)(2,1)}, u32[]{:S(2)}) copy-start(bf16[4,256,384]{2,1,0:T(8,128)(2,1)} %param.5) | copy-start | bytes 2359300
  6.5 52.5 %copy-start.6 = (f32[4,256]{1,0:T(4,128)S(1)}, f32[4,256]{1,0:T(4,128)}, u32[]{:S(2)}) copy-start(f32[4,256]{1,0:T(4,128)} %param.6) | copy-start | bytes 12292
  6.5 50.1 %all-gather.4.cloned.1.call-start = ((), (), s32[]{:S(2)}) async-start(), calls=%async_computation.4 | async-start | bytes 1114112 | tf_op jit(solution)/shard_map/all_gather | solution.py:21
  11.4 211.4 %reduce-scatter.5.cloned.1.call-start = ((), (), s32[]{:S(2)}) async-start(), calls=%async_computation.5 | async-start | bytes 17825792 | tf_op jit(solution)/shard_map/reduce_scatter | solution.py:41
  112.3 112.7 %copy-start.2 = (bf16[2048,256]{1,0:T(8,128)(2,1)S(1)}, bf16[2048,256]{1,0:T(8,128)(2,1)}, u32[]{:S(2)}) copy-start(bf16[2048,256]{1,0:T(8,128)(2,1)} %all-gather.4.cloned.1.call-done) | copy-start | bytes 3145732
  112.4 148.6 %reduce-scatter.7.cloned.1.call-start = ((), (), s32[]{:S(2)}) async-start(), calls=%async_computation.6 | async-start | bytes 1179648 | tf_op jit(solution)/shard_map/reduce_scatter | solution.py:57
  225.0 36.0 %copy-start.3 = (bf16[128,256]{1,0:T(8,128)(2,1)S(1)}, bf16[128,256]{1,0:T(8,128)(2,1)}, u32[]{:S(2)}) copy-start(bf16[128,256]{1,0:T(8,128)(2,1)} %param.9) | copy-start | bytes 196612
  229.5 74.9 %all-gather.6.cloned.1.call-start = ((), (), s32[]{:S(2)}) async-start(), calls=%async_computation.7 | async-start | bytes 1114112 | tf_op jit(solution)/shard_map/all_gather | solution.py:54
  262.6 78.1 %copy-start.1 = (bf16[128,256]{1,0:T(8,128)(2,1)S(1)}, bf16[128,256]{1,0:T(8,128)(2,1)}, u32[]{:S(2)}) copy-start(bf16[128,256]{1,0:T(8,128)(2,1)} %fusion.4) | copy-start | bytes 196612
  262.6 78.1 %reduce-scatter.9.cloned.1.call-start = ((), (), s32[]{:S(2)}) async-start(), calls=%async_computation.8 | async-start | bytes 1179648 | tf_op jit(solution)/shard_map/reduce_scatter | solution.py:57
  309.2 75.1 %all-gather.8.cloned.1.call-start = ((), (), s32[]{:S(2)}) async-start(), calls=%async_computation.9 | async-start | bytes 1114112 | tf_op jit(solution)/shard_map/all_gather | solution.py:54
  342.3 78.2 %copy-start.4 = (bf16[128,256]{1,0:T(8,128)(2,1)S(1)}, bf16[128,256]{1,0:T(8,128)(2,1)}, u32[]{:S(2)}) copy-start(bf16[128,256]{1,0:T(8,128)(2,1)} %fusion.5) | copy-start | bytes 196612
  342.3 78.2 %reduce-scatter.11.cloned.1.call-start = ((), (), s32[]{:S(2)}) async-start(), calls=%async_computation.10 | async-start | bytes 1179648 | tf_op jit(solution)/shard_map/reduce_scatter | solution.py:57
Sparse Core Ops, SparseCore 0:
  11.5 45.1 all-gather.3
  112.5 110.1 reduce-scatter.4
  229.6 31.3 reduce-scatter.6
  263.0 41.4 all-gather.5
  309.3 31.3 reduce-scatter.8
  342.7 41.4 all-gather.7
  389.1 31.3 reduce-scatter.10
where the time goes:
time: 430 us; the launch traced here: 429 us
  waiting for transfers between devices  333 us (77%)
  local copies, waits for them, and re-layouts  50.1 us (12%)
  other arithmetic  16.2 us (4%)
  matrix products  15.3 us (4%)
  between operations  13.6 us (3%)
    reduce_scatter x1, waiting for transfers between devices, body(): lax.psum_scatter(dense_local, 'row', scatter_dimension=0, tiled=True)  110 us
    reduce_scatter x3, waiting for transfers between devices, filter_step(): lax.psum_scatter(partial_value, 'col', scatter_dimension=0, tiled=True)  94.4 us
    all_gather x2, waiting for transfers between devices, times_ham(): return add_piece(lax.all_gather(vectors, 'row', axis=0, tiled=True))  83.7 us
    all_gather x1, waiting for transfers between devices, body(): group_orbitals = lax.all_gather(orbitals, 'row', axis=0, tiled=True)  44.9 us
    unnamed x16, local copies, waits for them, and re-layouts  16 us
    scatter-add x1, local copies, waits for them, and re-layouts, body(): dense_local = jnp.zeros((group_tiles, TILE, group_tiles, TILE), jnp.float...  15.5 us
    dot_general x2, matrix products, add_piece(): return jnp.dot(hamiltonian, piece, preferred_element_type=jnp.float32)  9.42 us
    scatter-add x1, other arithmetic, body(): dense_local = jnp.zeros((group_tiles, TILE, group_tiles, TILE), jnp.float...  9.09 us
  transfers between devices with their start and end apart: 7, of which 7 were waited for; matrix products, arithmetic and copies ran while one was open for 0% of the time, Pallas kernels for 0%

commit v1 on v0

v1 whole, which is shorter than its diff:
```python
import jax
import jax.numpy as jnp
from jax import lax
from jax.experimental import pallas as pl
from jax.experimental.pallas import tpu as pltpu
from jax.sharding import PartitionSpec as P

MESH = pl.DeviceIdType.MESH
TILE = 128
NORB = 256
LISTED = 3
BATCH = 4
PTS = 256
LIST = 384
SLOTS = BATCH * LISTED
HALF = TILE // 2
FAR = (2, 1, 3)
NEAR = (1, 3, 2)
BF = jnp.bfloat16
F32 = jnp.float32
center = 1.0
spread = 2.5


def kernel(
    tiles_ref, ext_ref, g_hbm, k_hbm, orb_hbm, out_ref,
    kin, g, gt, v, sb, r1, r2, cb, cr, pot, yb, inv,
    load_sem, ag_s, ag_r, r1_s, r1_r, r2_s, r2_r, c_s, c_r,
):
    row, col = lax.axis_index("row"), lax.axis_index("col")
    y, z = row // 4, row % 4
    x, core = col // 2, col % 2

    def at(dy, dz):
        return lax.rem(y + dy, 4) * 4 + lax.rem(z + dz, 4)

    def tile_of(h, p, q):
        return at(q, p) if h == 0 else at(p, q)

    load_k = pltpu.make_async_copy(k_hbm, kin, load_sem.at[0])
    load_g = pltpu.make_async_copy(g_hbm, g, load_sem.at[1])
    load_v = pltpu.make_async_copy(orb_hbm, v.at[0, row], load_sem.at[2])
    load_v.start()
    load_g.start()
    load_k.start()

    barrier = pltpu.get_barrier_semaphore()
    peers = [(at(0, d), col) for d in NEAR] + [(at(d, 0), col) for d in NEAR]
    peers += [(row, lax.rem(col + d, 8)) for d in range(1, 8)]
    for peer in peers:
        pl.semaphore_signal(barrier, inc=1, device_id=peer, device_id_type=MESH)

    def invert(u, carry):
        first, second = jnp.int32(SLOTS), jnp.int32(SLOTS)
        for s in range(SLOTS):
            hit = tiles_ref[s // LISTED, s % LISTED] == u
            second = jnp.where(hit & (first < SLOTS), s, second)
            first = jnp.where(hit & (first == SLOTS), s, first)
        inv[0, u] = first
        inv[1, u] = second
        return carry

    lax.fori_loop(0, 16, invert, 0)
    yb[SLOTS] = jnp.zeros((TILE, NORB), F32)
    pl.semaphore_wait(barrier, len(peers))
    load_v.wait()

    def gather(k):
        sends = []

        def send(h, p, q, dp, dq):
            part = v.at[k, tile_of(h, p, q), pl.ds(h * HALF, HALF)]
            rp, rq = (p - dp) % 4, (q - dq) % 4
            copy = pltpu.make_async_remote_copy(
                src_ref=part,
                dst_ref=part,
                send_sem=ag_s.at[h, rp, rq],
                recv_sem=ag_r.at[k, h, rp, rq],
                device_id=(tile_of(h, dp, dq), col),
                device_id_type=MESH,
            )
            copy.start()
            sends.append(copy)

        def arrive(h, p, q):
            part = v.at[k, tile_of(h, p, q), pl.ds(h * HALF, HALF)]
            pltpu.make_async_remote_copy(
                src_ref=part, dst_ref=part, send_sem=ag_s.at[h, p, q], recv_sem=ag_r.at[k, h, p, q],
                device_id=(row, col), device_id_type=MESH,
            ).wait_recv()

        for d in NEAR:
            for h in range(2):
                send(h, 0, 0, d, 0)
        for d in NEAR:
            for h in range(2):
                send(h, 0, 0, 0, d)
        for p in NEAR:
            for h in range(2):
                arrive(h, p, 0)
                for d in NEAR:
                    send(h, p, 0, 0, d)
        return sends, arrive

    def arrive_all(arrive):
        for p in (0, *NEAR):
            for q in NEAR:
                for h in range(2):
                    arrive(h, p, q)

    def waves_of(k, b):
        listed = jnp.concatenate([v[k, tiles_ref[b, s]] for s in range(LISTED)], axis=0)
        return jnp.dot(g[b], listed, preferred_element_type=F32)

    def scatter(k):
        sends, built = [], set()

        def build(dy, dz):
            if (dy, dz) in built:
                return
            built.add((dy, dz))
            u = at(dy, dz)
            sb[k, u] = (yb[inv[0, u]] + yb[inv[1, u]]).astype(BF)

        for q in (*FAR, 0):
            for d in FAR:
                build(q, d)
                build(d, q)
                for h in range(2):
                    rp = (-d) % 4
                    copy = pltpu.make_async_remote_copy(
                        src_ref=sb.at[k, tile_of(h, d, q), pl.ds(h * HALF, HALF)],
                        dst_ref=r1.at[k, h, q, rp],
                        send_sem=r1_s.at[h, q, rp],
                        recv_sem=r1_r.at[k, h, q, rp],
                        device_id=(tile_of(h, d, 0), col),
                        device_id_type=MESH,
                    )
                    copy.start()
                    sends.append(copy)
        build(0, 0)
        return sends

    def kinetic(k):
        sends = []
        vectors = v[k].reshape(16 * TILE, NORB)
        for dx in (*FAR, 0):
            there = lax.rem(x + dx, 4)
            rows = pl.ds(pl.multiple_of(there * 256, 256), 256)
            part = jnp.dot(kin[rows, :], vectors, preferred_element_type=F32)
            cb[k, there] = part.astype(BF).reshape(2, TILE, NORB)
            if dx == 0:
                targets = [1 - core]
            else:
                targets = [0, 1]
            for n, e in enumerate(targets):
                rx = (-dx) % 4
                copy = pltpu.make_async_remote_copy(
                    src_ref=cb.at[k, there, e],
                    dst_ref=cr.at[k, rx, core],
                    send_sem=c_s.at[dx, n],
                    recv_sem=c_r.at[k, rx, core],
                    device_id=(row, there * 2 + e),
                    device_id_type=MESH,
                )
                copy.start()
                sends.append(copy)
        return sends

    def pass_on(k):
        sends, kept = [], []
        for q in (*FAR, 0):
            for h in range(2):
                total = sb[k, tile_of(h, 0, q), pl.ds(h * HALF, HALF)].astype(F32)
                for p in FAR:
                    pltpu.make_async_remote_copy(
                        src_ref=r1.at[k, h, q, p], dst_ref=r1.at[k, h, q, p], send_sem=r1_s.at[h, q, p],
                        recv_sem=r1_r.at[k, h, q, p], device_id=(row, col), device_id_type=MESH,
                    ).wait_recv()
                    total = total + r1[k, h, q, p].astype(F32)
                if q == 0:
                    kept.append(total)
                    continue
                own = sb.at[k, tile_of(h, 0, q), pl.ds(h * HALF, HALF)]
                own[...] = total.astype(BF)
                rq = (-q) % 4
                copy = pltpu.make_async_remote_copy(
                    src_ref=own,
                    dst_ref=r2.at[k, h, rq],
                    send_sem=r2_s.at[h, rq],
                    recv_sem=r2_r.at[k, h, rq],
                    device_id=(tile_of(h, 0, q), col),
                    device_id_type=MESH,
                )
                copy.start()
                sends.append(copy)
        return sends, kept

    def collect(k, kept):
        total = cb[k, x, core].astype(F32)
        for dx in (0, *NEAR):
            for e in [1 - core] if dx == 0 else [0, 1]:
                pltpu.make_async_remote_copy(
                    src_ref=cr.at[k, dx, e], dst_ref=cr.at[k, dx, e], send_sem=c_s.at[0, 0],
                    recv_sem=c_r.at[k, dx, e], device_id=(row, col), device_id_type=MESH,
                ).wait_recv()
                total = total + cr[k, dx, e].astype(F32)
        halves = []
        for h in range(2):
            part = kept[h]
            for q in NEAR:
                pltpu.make_async_remote_copy(
                    src_ref=r2.at[k, h, q], dst_ref=r2.at[k, h, q], send_sem=r2_s.at[h, q],
                    recv_sem=r2_r.at[k, h, q], device_id=(row, col), device_id_type=MESH,
                ).wait_recv()
                part = part + r2[k, h, q].astype(F32)
            halves.append(part)
        return total + jnp.concatenate(halves, axis=0)

    for k in range(3):
        sends, arrive = gather(k)
        if k == 0:
            load_g.wait()
            for b in range(BATCH):
                gt[b] = g[b].T
            ext = ext_ref[...]
            ext = jnp.concatenate([ext, ext], axis=0).T
        arrive_all(arrive)
        for b in range(BATCH):
            waves = waves_of(k, b)
            if k == 0:
                density = jnp.sum(waves * waves, axis=1, keepdims=True)
                root = jnp.exp(jnp.log(density * (3.0 / jnp.pi)) * (1.0 / 3.0))
                pot[b] = jnp.broadcast_to(ext[:, b : b + 1] - root, (PTS, NORB))
            term = (pot[b] * waves).astype(BF)
            yb[pl.ds(b * LISTED, LISTED)] = jnp.dot(gt[b], term, preferred_element_type=F32).reshape(
                LISTED, TILE, NORB
            )
        sends += scatter(k)
        if k == 0:
            load_k.wait()
        sends += kinetic(k)
        more, kept = pass_on(k)
        sends += more
        product = collect(k, kept)
        own = v[k, row].astype(F32)
        applied = product / spread - (center / spread) * own
        if k == 0:
            v[1, row] = applied.astype(BF)
        else:
            result = 2.0 * applied - v[k - 1, row].astype(F32)
            if k == 1:
                v[2, row] = result.astype(BF)
            else:
                out_ref[...] = result
        for copy in sends:
            copy.wait_send()


def body(grid_values, external, tiles, kinetic, orbitals):
    any_spec = pl.BlockSpec(memory_space=pl.ANY)
    dma = pltpu.SemaphoreType.DMA
    return pl.pallas_call(
        kernel,
        out_shape=jax.ShapeDtypeStruct((TILE, NORB), F32),
        in_specs=[
            pl.BlockSpec(memory_space=pltpu.SMEM),
            pl.BlockSpec(memory_space=pltpu.VMEM),
            any_spec,
            any_spec,
            any_spec,
        ],
        out_specs=pl.BlockSpec(memory_space=pltpu.VMEM),
        scratch_shapes=[
            pltpu.VMEM(kinetic.shape, BF),
            pltpu.VMEM((BATCH, PTS, LIST), BF),
            pltpu.VMEM((BATCH, LIST, PTS), BF),
            pltpu.VMEM((3, 16, TILE, NORB), BF),
            pltpu.VMEM((3, 16, TILE, NORB), BF),
            pltpu.VMEM((3, 2, 4, 4, HALF, NORB), BF),
            pltpu.VMEM((3, 2, 4, HALF, NORB), BF),
            pltpu.VMEM((3, 4, 2, TILE, NORB), BF),
            pltpu.VMEM((3, 4, 2, TILE, NORB), BF),
            pltpu.VMEM((BATCH, PTS, NORB), F32),
            pltpu.VMEM((SLOTS + 1, TILE, NORB), F32),
            pltpu.SMEM((2, 16), jnp.int32),
            dma((3,)),
            dma((2, 4, 4)),
            dma((3, 2, 4, 4)),
            dma((2, 4, 4)),
            dma((3, 2, 4, 4)),
            dma((2, 4)),
            dma((3, 2, 4)),
            dma((4, 2)),
            dma((3, 4, 2)),
        ],
        compiler_params=pltpu.CompilerParams(
            collective_id=0, has_side_effects=True, vmem_limit_bytes=60 * 1024 * 1024
        ),
    )(tiles, external, grid_values, kinetic, orbitals)


def solution(mesh):
    return jax.shard_map(
        body,
        mesh=mesh,
        in_specs=(
            P(("row", "col"), None, None),
            P(("row", "col"), None),
            P(("row", "col"), None),
            P("row", "col"),
            P(("row", "col"), None),
        ),
        out_specs=P(("row", "col"), None),
        check_vma=False,
    )
```

time: 430 us -> 77.2 us (0.18)
  waiting for transfers between devices: 333 us -> 0 us
  Pallas kernels: 0 us -> 75.5 us
  local copies, waits for them, and re-layouts: 50.1 us -> 1.57 us
  other arithmetic: 16.2 us -> 0 us
  matrix products: 15.3 us -> 0 us
  between operations: 13.6 us -> 0.01 us
    reduce_scatter x4 -> x0, waiting for transfers between devices: 205 us -> none  [the longest x1 110 us: body(): lax.psum_scatter(dense_local, 'row', scatter_dimension=0, tiled=True)]
    all_gather x3 -> x0, waiting for transfers between devices: 129 us -> none  [the longest x2 83.7 us: times_ham(): return add_piece(lax.all_gather(vectors, 'row', axis=0, tiled=True))]
    pallas_call x0 -> x1, Pallas kernels: none -> 75.5 us  [body(): pl.pallas_call(kernel, out_shape=jax.ShapeDtypeStruct((TILE, NORB), F32),...]
    scatter-add x1 -> x0, local copies, waits for them, and re-layouts: 15.5 us -> none  [body(): dense_local = jnp.zeros((group_tiles, TILE, group_tiles, TILE), jnp.float...]
    dot_general x5 -> x0, matrix products: 15.3 us -> none  [the longest x2 9.42 us: add_piece(): return jnp.dot(hamiltonian, piece, preferred_element_type=jnp.float32)]
    unnamed x16 -> x1, local copies, waits for them, and re-layouts: 16 us -> 1.57 us
    scatter-add x1 -> x0, other arithmetic: 9.09 us -> none  [body(): dense_local = jnp.zeros((group_tiles, TILE, group_tiles, TILE), jnp.float...]
    broadcast_in_dim x2 -> x0, local copies, waits for them, and re-layouts: 7.96 us -> none  [the longest x1 7.88 us: body(): jnp.zeros((group_tiles, TILE, group_tiles, TILE), jnp.float32)]
  transfers between devices with their start and end apart: 7 -> 0, of which waited for: 7 -> 0; matrix products, arithmetic and copies ran while one was open for 0% -> 0% of each run, Pallas kernels for 0% -> 0%
where the time goes in v1:
time: 77.2 us; the launch traced here: 77 us
  Pallas kernels  75.5 us (98%)
  local copies, waits for them, and re-layouts  1.57 us (2%)
    pallas_call x1, Pallas kernels, body(): pl.pallas_call(kernel, out_shape=jax.ShapeDtypeStruct((TILE, NORB), F32),...  75.5 us
    unnamed x1, local copies, waits for them, and re-layouts  1.57 us

profile of v1, /device:TPU:0, one launch (start us, length us, event | category | flops | bytes accessed | tf_op | source)
XLA Modules:
  0.0 77.0 jit_solution(9720695320154709849)
XLA Ops:
  0.0 75.5 %shard_map.55 = f32[128,256]{1,0:T(8,128)} custom-call(s32[4,3]{1,0:T(4,128)} %tiles_ref.1, f32[4,256]{1,0:T(4,128)} %ext_ref.1, bf16[4,256,384]{2,1,0:T(8,128)(2,1)} %g_hbm.1, bf16[1024,2048]{1,0:T(8,128)(2,1)} %k_hbm.1, bf16[128,256]{1,0:T(8,128)(2,1)} %orb_hbm.1), custom_call_target="tpu_custom_call" | custom-call | tf_op jit(solution)/shard_map/pallas_call | solution.py:263
  75.5 1.6 %copy.7 = f32[128,256]{1,0:T(8,128)} copy(f32[128,256]{1,0:T(8,128)} %shard_map.55) | data formatting | bytes 262144

commit v2 on v0

v2 whole, which is shorter than its diff:
```python
import jax
import jax.numpy as jnp
from jax import lax
from jax.experimental import pallas as pl
from jax.experimental.pallas import tpu as pltpu
from jax.sharding import PartitionSpec as P

MESH = pl.DeviceIdType.MESH
TILE = 128
STREAMS = 2
LANES = 128
LISTED = 3
BATCH = 4
PTS = 256
LIST = 384
SLOTS = BATCH * LISTED
HALF = TILE // 2
FAR = (2, 1, 3)
NEAR = (1, 3, 2)
BF = jnp.bfloat16
F32 = jnp.float32
center = 1.0
spread = 2.5


def kernel(
    tiles_ref, ext_ref, g_hbm, k_hbm, orb_hbm, out_ref,
    kin, g, gt, v_one, v_two, sb, r1, r2, cb, cr, pot, yb, inv,
    load_sem, near_r, far_r, rest_r, r1_r, r2_r, c_r, ag_s, r1_s, r2_s, c_s,
):
    v = (v_one, v_two)
    row, col = lax.axis_index("row"), lax.axis_index("col")
    y, z = row // 4, row % 4
    x, core = col // 2, col % 2

    def at(dy, dz):
        return lax.rem(y + dy, 4) * 4 + lax.rem(z + dz, 4)

    def tile_of(h, p, q):
        return at(q, p) if h == 0 else at(p, q)

    def start(src, dst, send, recv, target):
        pltpu.make_async_remote_copy(
            src_ref=src, dst_ref=dst, send_sem=send, recv_sem=recv, device_id=target, device_id_type=MESH
        ).start()

    def arrived(ref, recv):
        pltpu.make_async_remote_copy(
            src_ref=ref, dst_ref=ref, send_sem=recv, recv_sem=recv, device_id=(row, col), device_id_type=MESH
        ).wait_recv()

    def sent(ref, send):
        pltpu.make_async_remote_copy(
            src_ref=ref, dst_ref=ref, send_sem=send, recv_sem=send, device_id=(row, col), device_id_type=MESH
        ).wait_send()

    load_k = pltpu.make_async_copy(k_hbm, kin, load_sem.at[0])
    load_g = pltpu.make_async_copy(g_hbm, g, load_sem.at[1])
    load_v = [
        pltpu.make_async_copy(orb_hbm.at[:, pl.ds(s * LANES, LANES)], v[s].at[0, row], load_sem.at[2 + s])
        for s in range(STREAMS)
    ]
    for load in load_v:
        load.start()
    load_g.start()
    load_k.start()

    barrier = pltpu.get_barrier_semaphore()
    peers = [(at(0, d), col) for d in NEAR] + [(at(d, 0), col) for d in NEAR]
    peers += [(row, lax.rem(col + d, 8)) for d in range(1, 8)]
    for peer in peers:
        pl.semaphore_signal(barrier, inc=1, device_id=peer, device_id_type=MESH)

    def invert(u, carry):
        first, second = jnp.int32(SLOTS), jnp.int32(SLOTS)
        for n in range(SLOTS):
            hit = tiles_ref[n // LISTED, n % LISTED] == u
            second = jnp.where(hit & (first < SLOTS), n, second)
            first = jnp.where(hit & (first == SLOTS), n, first)
        inv[0, u] = first
        inv[1, u] = second
        return carry

    lax.fori_loop(0, 16, invert, 0)
    for s in range(STREAMS):
        yb[s, SLOTS] = jnp.zeros((TILE, LANES), F32)
    pl.semaphore_wait(barrier, len(peers))
    for load in load_v:
        load.wait()

    def pass_tile(k, s, h, p, q, dp, dq):
        part = v[s].at[k, tile_of(h, p, q), pl.ds(h * HALF, HALF)]
        if dq:
            recv = rest_r.at[k, s]
        else:
            recv = far_r.at[k, s] if dp == 2 else near_r.at[k, s]
        start(part, part, ag_s.at[s], recv, (tile_of(h, dp, dq), col))

    def gather_own(k, s):
        for d in NEAR:
            for h in range(2):
                pass_tile(k, s, h, 0, 0, d, 0)
        for d in NEAR:
            for h in range(2):
                pass_tile(k, s, h, 0, 0, 0, d)

    def gather_rest(k, s):
        arrived(v[s].at[k, pl.ds(0, 2)], near_r.at[k, s])
        for p in (1, 3):
            for d in NEAR:
                for h in range(2):
                    pass_tile(k, s, h, p, 0, 0, d)
        arrived(v[s].at[k, 0], far_r.at[k, s])
        for d in NEAR:
            for h in range(2):
                pass_tile(k, s, h, 2, 0, 0, d)

    def gathered(k, s):
        arrived(v[s].at[k, pl.ds(0, 12)], rest_r.at[k, s])

    def listed(k, s, b):
        return jnp.concatenate([v[s][k, tiles_ref[b, n]] for n in range(LISTED)], axis=0)

    def grid_first(ext):
        for b in range(BATCH):
            both = jnp.concatenate([listed(0, s, b) for s in range(STREAMS)], axis=1)
            waves = jnp.dot(g[b], both, preferred_element_type=F32)
            density = jnp.sum(waves * waves, axis=1, keepdims=True)
            root = jnp.exp(jnp.log(density * (3.0 / jnp.pi)) * (1.0 / 3.0))
            value = jnp.broadcast_to(ext[:, b : b + 1] - root, (PTS, LANES))
            pot[b] = value
            term = (jnp.concatenate([value] * STREAMS, axis=1) * waves).astype(BF)
            sums = jnp.dot(gt[b], term, preferred_element_type=F32)
            for s in range(STREAMS):
                part = sums[:, s * LANES : (s + 1) * LANES]
                yb[s, pl.ds(b * LISTED, LISTED)] = part.reshape(LISTED, TILE, LANES)

    def grid(k, s):
        for b in range(BATCH):
            waves = jnp.dot(g[b], listed(k, s, b), preferred_element_type=F32)
            term = (pot[b] * waves).astype(BF)
            sums = jnp.dot(gt[b], term, preferred_element_type=F32)
            yb[s, pl.ds(b * LISTED, LISTED)] = sums.reshape(LISTED, TILE, LANES)

    def scatter(k, s):
        built = set()

        def build(dy, dz):
            if (dy, dz) in built:
                return
            built.add((dy, dz))
            u = at(dy, dz)
            sb[s, k, u] = (yb[s, inv[0, u]] + yb[s, inv[1, u]]).astype(BF)

        for q in (*FAR, 0):
            for d in FAR:
                build(q, d)
                build(d, q)
                for h in range(2):
                    start(
                        sb.at[s, k, tile_of(h, d, q), pl.ds(h * HALF, HALF)],
                        r1.at[s, k, q, h, 3 - d],
                        r1_s.at[s],
                        r1_r.at[k, s, q],
                        (tile_of(h, d, 0), col),
                    )
        build(0, 0)

    def kinetic(k):
        def block(n, carry):
            rows = pl.ds(pl.multiple_of(n * 256, 256), 256)
            both = jnp.concatenate([v[s][k].reshape(16 * TILE, LANES) for s in range(STREAMS)], axis=1)
            part = jnp.dot(kin[rows, :], both, preferred_element_type=F32).astype(BF)
            for s in range(STREAMS):
                cb[s, k, pl.ds(2 * n, 2)] = part[:, s * LANES : (s + 1) * LANES].reshape(2, TILE, LANES)
            return carry

        lax.fori_loop(0, 4, block, 0)
        other = x * 2 + 1 - core
        for s in range(STREAMS):
            for dx in FAR:
                there = lax.rem(x + dx, 4)
                for e in range(2):
                    start(
                        cb.at[s, k, there * 2 + e],
                        cr.at[s, k, (3 - dx) * 2 + core],
                        c_s.at[s],
                        c_r.at[k, s],
                        (row, there * 2 + e),
                    )
            start(cb.at[s, k, other], cr.at[s, k, 6], c_s.at[s], c_r.at[k, s], (row, other))

    def pass_on(k, s):
        kept = []
        for q in (*FAR, 0):
            arrived(r1.at[s, k, q], r1_r.at[k, s, q])
            for h in range(2):
                own = sb.at[s, k, tile_of(h, 0, q), pl.ds(h * HALF, HALF)]
                total = own[...].astype(F32)
                for n in range(3):
                    total = total + r1[s, k, q, h, n].astype(F32)
                if q == 0:
                    kept.append(total)
                    continue
                own[...] = total.astype(BF)
                start(own, r2.at[s, k, h, 3 - q], r2_s.at[s], r2_r.at[k, s], (tile_of(h, 0, q), col))
        return jnp.concatenate(kept, axis=0)

    def collect(k, s, kept):
        arrived(cr.at[s, k], c_r.at[k, s])
        total = kept + cb[s, k, col].astype(F32)
        for n in range(7):
            total = total + cr[s, k, n].astype(F32)
        arrived(r2.at[s, k], r2_r.at[k, s])
        total = total + sum(
            jnp.concatenate([r2[s, k, h, n].astype(F32) for h in range(2)], axis=0) for n in range(3)
        )
        applied = total / spread - (center / spread) * v[s][k, row].astype(F32)
        if k == 0:
            v[s][1, row] = applied.astype(BF)
            return
        result = 2.0 * applied - v[s][k - 1, row].astype(F32)
        if k == 1:
            v[s][2, row] = result.astype(BF)
        else:
            out_ref[:, pl.ds(s * LANES, LANES)] = result

    kept = {}

    def step(name, k, s):
        with jax.named_scope(f"{name}{k}{s}"):
            if name == "own":
                gather_own(k, s)
            elif name == "rest":
                gather_rest(k, s)
            elif name == "wait":
                gathered(k, s)
            elif name == "grid":
                grid(k, s)
                scatter(k, s)
            elif name == "scat":
                scatter(k, s)
            elif name == "kin":
                kinetic(k)
            elif name == "pass":
                kept[k, s] = pass_on(k, s)
            elif name == "coll":
                collect(k, s, kept[k, s])

    step("own", 0, 0)
    step("own", 0, 1)
    with jax.named_scope("prep"):
        load_g.wait()
        for b in range(BATCH):
            gt[b] = g[b].T
        ext = ext_ref[...]
        ext = jnp.concatenate([ext, ext], axis=0).T
    step("rest", 0, 0)
    step("rest", 0, 1)
    step("wait", 0, 0)
    step("wait", 0, 1)
    with jax.named_scope("first"):
        grid_first(ext)
    for k in range(3):
        if k == 0:
            step("scat", 0, 0)
            step("scat", 0, 1)
            load_k.wait()
        else:
            step("rest", k, 0)
            step("rest", k, 1)
            step("wait", k, 0)
            step("grid", k, 0)
            step("wait", k, 1)
            step("grid", k, 1)
        step("kin", k, 0)
        step("pass", k, 0)
        step("pass", k, 1)
        step("coll", k, 0)
        if k < 2:
            step("own", k + 1, 0)
        step("coll", k, 1)
        if k < 2:
            step("own", k + 1, 1)

    for s in range(STREAMS):
        sent(v[s].at[:, pl.ds(0, 15)], ag_s.at[s])
        sent(r1.at[s], r1_s.at[s])
        sent(r2.at[s], r2_s.at[s])
        sent(cr.at[s], c_s.at[s])


def body(grid_values, external, tiles, kinetic, orbitals):
    any_spec = pl.BlockSpec(memory_space=pl.ANY)
    dma = pltpu.SemaphoreType.DMA
    return pl.pallas_call(
        kernel,
        out_shape=jax.ShapeDtypeStruct((TILE, STREAMS * LANES), F32),
        in_specs=[
            pl.BlockSpec(memory_space=pltpu.SMEM),
            pl.BlockSpec(memory_space=pltpu.VMEM),
            any_spec,
            any_spec,
            any_spec,
        ],
        out_specs=pl.BlockSpec(memory_space=pltpu.VMEM),
        scratch_shapes=[
            pltpu.VMEM(kinetic.shape, BF),
            pltpu.VMEM((BATCH, PTS, LIST), BF),
            pltpu.VMEM((BATCH, LIST, PTS), BF),
            pltpu.VMEM((3, 16, TILE, LANES), BF),
            pltpu.VMEM((3, 16, TILE, LANES), BF),
            pltpu.VMEM((STREAMS, 3, 16, TILE, LANES), BF),
            pltpu.VMEM((STREAMS, 3, 4, 2, 3, HALF, LANES), BF),
            pltpu.VMEM((STREAMS, 3, 2, 3, HALF, LANES), BF),
            pltpu.VMEM((STREAMS, 3, 8, TILE, LANES), BF),
            pltpu.VMEM((STREAMS, 3, 7, TILE, LANES), BF),
            pltpu.VMEM((BATCH, PTS, LANES), F32),
            pltpu.VMEM((STREAMS, SLOTS + 1, TILE, LANES), F32),
            pltpu.SMEM((2, 16), jnp.int32),
            dma((2 + STREAMS,)),
            dma((3, STREAMS)),
            dma((3, STREAMS)),
            dma((3, STREAMS)),
            dma((3, STREAMS, 4)),
            dma((3, STREAMS)),
            dma((3, STREAMS)),
            dma((STREAMS,)),
            dma((STREAMS,)),
            dma((STREAMS,)),
            dma((STREAMS,)),
        ],
        compiler_params=pltpu.CompilerParams(
            collective_id=0, has_side_effects=True, vmem_limit_bytes=60 * 1024 * 1024
        ),
    )(tiles, external, grid_values, kinetic, orbitals)


def solution(mesh):
    return jax.shard_map(
        body,
        mesh=mesh,
        in_specs=(
            P(("row", "col"), None, None),
            P(("row", "col"), None),
            P(("row", "col"), None),
            P("row", "col"),
            P(("row", "col"), None),
        ),
        out_specs=P(("row", "col"), None),
        check_vma=False,
    )
```

time: 430 us -> 71.5 us (0.17)
  waiting for transfers between devices: 333 us -> 0 us
  Pallas kernels: 0 us -> 68.6 us
  local copies, waits for them, and re-layouts: 50.1 us -> 1.57 us
  other arithmetic: 16.2 us -> 0 us
  matrix products: 15.3 us -> 0 us
  between operations: 13.6 us -> 0.01 us
    reduce_scatter x4 -> x0, waiting for transfers between devices: 205 us -> none  [the longest x1 110 us: body(): lax.psum_scatter(dense_local, 'row', scatter_dimension=0, tiled=True)]
    all_gather x3 -> x0, waiting for transfers between devices: 129 us -> none  [the longest x2 83.7 us: times_ham(): return add_piece(lax.all_gather(vectors, 'row', axis=0, tiled=True))]
    pallas_call x0 -> x1, Pallas kernels: none -> 68.6 us  [body(): pl.pallas_call(kernel, out_shape=jax.ShapeDtypeStruct((TILE, STREAMS * LA...]
    scatter-add x1 -> x0, local copies, waits for them, and re-layouts: 15.5 us -> none  [body(): dense_local = jnp.zeros((group_tiles, TILE, group_tiles, TILE), jnp.float...]
    dot_general x5 -> x0, matrix products: 15.3 us -> none  [the longest x2 9.42 us: add_piece(): return jnp.dot(hamiltonian, piece, preferred_element_type=jnp.float32)]
    unnamed x16 -> x1, local copies, waits for them, and re-layouts: 16 us -> 1.57 us
    scatter-add x1 -> x0, other arithmetic: 9.09 us -> none  [body(): dense_local = jnp.zeros((group_tiles, TILE, group_tiles, TILE), jnp.float...]
    broadcast_in_dim x2 -> x0, local copies, waits for them, and re-layouts: 7.96 us -> none  [the longest x1 7.88 us: body(): jnp.zeros((group_tiles, TILE, group_tiles, TILE), jnp.float32)]
  transfers between devices with their start and end apart: 7 -> 0, of which waited for: 7 -> 0; matrix products, arithmetic and copies ran while one was open for 0% -> 0% of each run, Pallas kernels for 0% -> 0%
where the time goes in v2:
time: 71.5 us; the launch traced here: 70.2 us
  Pallas kernels  68.6 us (96%)
  local copies, waits for them, and re-layouts  1.57 us (2%)
    pallas_call x1, Pallas kernels, body(): pl.pallas_call(kernel, out_shape=jax.ShapeDtypeStruct((TILE, STREAMS * LA...  68.6 us
    unnamed x1, local copies, waits for them, and re-layouts  1.57 us

profile of v2, /device:TPU:0, one launch (start us, length us, event | category | flops | bytes accessed | tf_op | source)
XLA Modules:
  0.0 70.2 jit_solution(16962003520523341874)
XLA Ops:
  0.0 68.6 %shard_map.55 = f32[128,256]{1,0:T(8,128)} custom-call(s32[4,3]{1,0:T(4,128)} %tiles_ref.1, f32[4,256]{1,0:T(4,128)} %ext_ref.1, bf16[4,256,384]{2,1,0:T(8,128)(2,1)} %g_hbm.1, bf16[1024,2048]{1,0:T(8,128)(2,1)} %k_hbm.1, bf16[128,256]{1,0:T(8,128)(2,1)} %orb_hbm.1), custom_call_target="tpu_custom_call" | custom-call | tf_op jit(solution)/shard_map/pallas_call | solution.py:296
  68.6 1.6 %copy.7 = f32[128,256]{1,0:T(8,128)} copy(f32[128,256]{1,0:T(8,128)} %shard_map.55) | data formatting | bytes 262144

commit v3 on v2

--- a/solution.py
+++ b/solution.py
@@ -24,8 +24,8 @@
 
 
 def kernel(
-    tiles_ref, ext_ref, g_hbm, k_hbm, orb_hbm, out_ref,
-    kin, g, gt, v_one, v_two, sb, r1, r2, cb, cr, pot, yb, inv,
+    tiles_hbm, ext_hbm, g_hbm, k_hbm, orb_hbm, out_ref,
+    kin, g, gt, v_one, v_two, sb, r1, r2, cb, cr, pot, yb, ext_ref, tiles_ref, inv,
     load_sem, near_r, far_r, rest_r, r1_r, r2_r, c_r, ag_s, r1_s, r2_s, c_s,
 ):
     v = (v_one, v_two)
@@ -54,22 +54,26 @@
             src_ref=ref, dst_ref=ref, send_sem=send, recv_sem=send, device_id=(row, col), device_id_type=MESH
         ).wait_send()
 
+    barrier = pltpu.get_barrier_semaphore()
+    peers = [(at(0, d), col) for d in NEAR] + [(at(d, 0), col) for d in NEAR]
+    peers += [(row, lax.rem(col + d, 8)) for d in range(1, 8)]
+    for peer in peers:
+        pl.semaphore_signal(barrier, inc=1, device_id=peer, device_id_type=MESH)
+
     load_k = pltpu.make_async_copy(k_hbm, kin, load_sem.at[0])
     load_g = pltpu.make_async_copy(g_hbm, g, load_sem.at[1])
     load_v = [
         pltpu.make_async_copy(orb_hbm.at[:, pl.ds(s * LANES, LANES)], v[s].at[0, row], load_sem.at[2 + s])
         for s in range(STREAMS)
     ]
+    load_ext = pltpu.make_async_copy(ext_hbm, ext_ref, load_sem.at[2 + STREAMS])
     for load in load_v:
         load.start()
+    load_ext.start()
+    load_tiles = pltpu.make_async_copy(tiles_hbm, tiles_ref, load_sem.at[3 + STREAMS])
+    load_tiles.start()
     load_g.start()
     load_k.start()
-
-    barrier = pltpu.get_barrier_semaphore()
-    peers = [(at(0, d), col) for d in NEAR] + [(at(d, 0), col) for d in NEAR]
-    peers += [(row, lax.rem(col + d, 8)) for d in range(1, 8)]
-    for peer in peers:
-        pl.semaphore_signal(barrier, inc=1, device_id=peer, device_id_type=MESH)
 
     def invert(u, carry):
         first, second = jnp.int32(SLOTS), jnp.int32(SLOTS)
@@ -81,6 +85,7 @@
         inv[1, u] = second
         return carry
 
+    load_tiles.wait()
     lax.fori_loop(0, 16, invert, 0)
     for s in range(STREAMS):
         yb[s, SLOTS] = jnp.zeros((TILE, LANES), F32)
@@ -97,21 +102,21 @@
         start(part, part, ag_s.at[s], recv, (tile_of(h, dp, dq), col))
 
     def gather_own(k, s):
-        for d in NEAR:
+        for d in FAR:
             for h in range(2):
                 pass_tile(k, s, h, 0, 0, d, 0)
-        for d in NEAR:
+        for d in FAR:
             for h in range(2):
                 pass_tile(k, s, h, 0, 0, 0, d)
 
     def gather_rest(k, s):
         arrived(v[s].at[k, pl.ds(0, 2)], near_r.at[k, s])
         for p in (1, 3):
-            for d in NEAR:
+            for d in FAR:
                 for h in range(2):
                     pass_tile(k, s, h, p, 0, 0, d)
         arrived(v[s].at[k, 0], far_r.at[k, s])
-        for d in NEAR:
+        for d in FAR:
             for h in range(2):
                 pass_tile(k, s, h, 2, 0, 0, d)
 
@@ -122,24 +127,32 @@
         return jnp.concatenate([v[s][k, tiles_ref[b, n]] for n in range(LISTED)], axis=0)
 
     def grid_first(ext):
+        terms = []
+        waves = [
+            jnp.dot(
+                g[b],
+                jnp.concatenate([listed(0, s, b) for s in range(STREAMS)], axis=1),
+                preferred_element_type=F32,
+            )
+            for b in range(BATCH)
+        ]
         for b in range(BATCH):
-            both = jnp.concatenate([listed(0, s, b) for s in range(STREAMS)], axis=1)
-            waves = jnp.dot(g[b], both, preferred_element_type=F32)
-            density = jnp.sum(waves * waves, axis=1, keepdims=True)
+            density = jnp.sum(waves[b] * waves[b], axis=1, keepdims=True)
             root = jnp.exp(jnp.log(density * (3.0 / jnp.pi)) * (1.0 / 3.0))
             value = jnp.broadcast_to(ext[:, b : b + 1] - root, (PTS, LANES))
             pot[b] = value
-            term = (jnp.concatenate([value] * STREAMS, axis=1) * waves).astype(BF)
-            sums = jnp.dot(gt[b], term, preferred_element_type=F32)
+            terms.append((jnp.concatenate([value] * STREAMS, axis=1) * waves[b]).astype(BF))
+        for b in range(BATCH):
+            sums = jnp.dot(gt[b], terms[b], preferred_element_type=F32)
             for s in range(STREAMS):
                 part = sums[:, s * LANES : (s + 1) * LANES]
                 yb[s, pl.ds(b * LISTED, LISTED)] = part.reshape(LISTED, TILE, LANES)
 
     def grid(k, s):
+        waves = [jnp.dot(g[b], listed(k, s, b), preferred_element_type=F32) for b in range(BATCH)]
+        terms = [(pot[b] * waves[b]).astype(BF) for b in range(BATCH)]
         for b in range(BATCH):
-            waves = jnp.dot(g[b], listed(k, s, b), preferred_element_type=F32)
-            term = (pot[b] * waves).astype(BF)
-            sums = jnp.dot(gt[b], term, preferred_element_type=F32)
+            sums = jnp.dot(gt[b], terms[b], preferred_element_type=F32)
             yb[s, pl.ds(b * LISTED, LISTED)] = sums.reshape(LISTED, TILE, LANES)
 
     def scatter(k, s):
@@ -166,29 +179,32 @@
                     )
         build(0, 0)
 
-    def kinetic(k):
+    def send_parts(k, s):
+        for dx in FAR:
+            there = lax.rem(x + dx, 4)
+            for e in range(2):
+                start(
+                    cb.at[s, k, there * 2 + e],
+                    cr.at[s, k, (3 - dx) * 2 + core],
+                    c_s.at[s],
+                    c_r.at[k, s],
+                    (row, there * 2 + e),
+                )
+        other = x * 2 + 1 - core
+        start(cb.at[s, k, other], cr.at[s, k, 6], c_s.at[s], c_r.at[k, s], (row, other))
+
+    def kinetic(k, streams):
         def block(n, carry):
             rows = pl.ds(pl.multiple_of(n * 256, 256), 256)
-            both = jnp.concatenate([v[s][k].reshape(16 * TILE, LANES) for s in range(STREAMS)], axis=1)
-            part = jnp.dot(kin[rows, :], both, preferred_element_type=F32).astype(BF)
-            for s in range(STREAMS):
-                cb[s, k, pl.ds(2 * n, 2)] = part[:, s * LANES : (s + 1) * LANES].reshape(2, TILE, LANES)
+            right = jnp.concatenate([v[s][k].reshape(16 * TILE, LANES) for s in streams], axis=1)
+            part = jnp.dot(kin[rows, :], right, preferred_element_type=F32).astype(BF)
+            for i, s in enumerate(streams):
+                cb[s, k, pl.ds(2 * n, 2)] = part[:, i * LANES : (i + 1) * LANES].reshape(2, TILE, LANES)
             return carry
 
         lax.fori_loop(0, 4, block, 0)
-        other = x * 2 + 1 - core
-        for s in range(STREAMS):
-            for dx in FAR:
-                there = lax.rem(x + dx, 4)
-                for e in range(2):
-                    start(
-                        cb.at[s, k, there * 2 + e],
-                        cr.at[s, k, (3 - dx) * 2 + core],
-                        c_s.at[s],
-                        c_r.at[k, s],
-                        (row, there * 2 + e),
-                    )
-            start(cb.at[s, k, other], cr.at[s, k, 6], c_s.at[s], c_r.at[k, s], (row, other))
+        for s in streams:
+            send_parts(k, s)
 
     def pass_on(k, s):
         kept = []
@@ -241,7 +257,7 @@
             elif name == "scat":
                 scatter(k, s)
             elif name == "kin":
-                kinetic(k)
+                kinetic(k, (0, 1) if k == 0 else (s,))
             elif name == "pass":
                 kept[k, s] = pass_on(k, s)
             elif name == "coll":
@@ -253,6 +269,7 @@
         load_g.wait()
         for b in range(BATCH):
             gt[b] = g[b].T
+        load_ext.wait()
         ext = ext_ref[...]
         ext = jnp.concatenate([ext, ext], axis=0).T
     step("rest", 0, 0)
@@ -266,14 +283,16 @@
             step("scat", 0, 0)
             step("scat", 0, 1)
             load_k.wait()
+            step("kin", 0, 0)
         else:
             step("rest", k, 0)
             step("rest", k, 1)
             step("wait", k, 0)
             step("grid", k, 0)
+            step("kin", k, 0)
             step("wait", k, 1)
             step("grid", k, 1)
-        step("kin", k, 0)
+            step("kin", k, 1)
         step("pass", k, 0)
         step("pass", k, 1)
         step("coll", k, 0)
@@ -297,8 +316,8 @@
         kernel,
         out_shape=jax.ShapeDtypeStruct((TILE, STREAMS * LANES), F32),
         in_specs=[
-            pl.BlockSpec(memory_space=pltpu.SMEM),
-            pl.BlockSpec(memory_space=pltpu.VMEM),
+            any_spec,
+            any_spec,
             any_spec,
             any_spec,
             any_spec,
@@ -317,8 +336,10 @@
             pltpu.VMEM((STREAMS, 3, 7, TILE, LANES), BF),
             pltpu.VMEM((BATCH, PTS, LANES), F32),
             pltpu.VMEM((STREAMS, SLOTS + 1, TILE, LANES), F32),
+            pltpu.VMEM((BATCH, PTS), F32),
+            pltpu.SMEM((BATCH, LISTED), jnp.int32),
             pltpu.SMEM((2, 16), jnp.int32),
-            dma((2 + STREAMS,)),
+            dma((4 + STREAMS,)),
             dma((3, STREAMS)),
             dma((3, STREAMS)),
             dma((3, STREAMS)),

time: 71.5 us -> 66 us (0.923); the launches traced: 70.2 us -> 65.9 us
  Pallas kernels: 68.6 us -> 64.3 us
    pallas_call x1, Pallas kernels: 68.6 us -> 64.3 us  [body(): pl.pallas_call(kernel, out_shape=jax.ShapeDtypeStruct((TILE, STREAMS * LA...]
where the time goes in v3:
time: 66 us; the launch traced here: 65.9 us
  Pallas kernels  64.3 us (97%)
  local copies, waits for them, and re-layouts  1.57 us (2%)
    pallas_call x1, Pallas kernels, body(): pl.pallas_call(kernel, out_shape=jax.ShapeDtypeStruct((TILE, STREAMS * LA...  64.3 us
    unnamed x1, local copies, waits for them, and re-layouts  1.57 us

profile of v3, /device:TPU:0, one launch (start us, length us, event | category | flops | bytes accessed | tf_op | source)
XLA Modules:
  0.0 65.9 jit_solution(2460760639498353878)
XLA Ops:
  0.0 64.3 %shard_map.55 = f32[128,256]{1,0:T(8,128)} custom-call(s32[4,3]{1,0:T(4,128)} %tiles_hbm.1, f32[4,256]{1,0:T(4,128)} %ext_hbm.1, bf16[4,256,384]{2,1,0:T(8,128)(2,1)} %g_hbm.1, bf16[1024,2048]{1,0:T(8,128)(2,1)} %k_hbm.1, bf16[128,256]{1,0:T(8,128)(2,1)} %orb_hbm.1), custom_call_target="tpu_custom_call" | custom-call | tf_op jit(solution)/shard_map/pallas_call | solution.py:315
  64.4 1.6 %copy.7 = f32[128,256]{1,0:T(8,128)} copy(f32[128,256]{1,0:T(8,128)} %shard_map.55) | data formatting | bytes 262144

commit v4 on v3

--- a/solution.py
+++ b/solution.py
@@ -24,7 +24,7 @@
 
 
 def kernel(
-    tiles_hbm, ext_hbm, g_hbm, k_hbm, orb_hbm, out_ref,
+    tiles_hbm, ext_hbm, g_hbm, k_hbm, orb_hbm, out_ref, prev_ref,
     kin, g, gt, v_one, v_two, sb, r1, r2, cb, cr, pot, yb, ext_ref, tiles_ref, inv,
     load_sem, near_r, far_r, rest_r, r1_r, r2_r, c_r, ag_s, r1_s, r2_s, c_s,
 ):
@@ -195,14 +195,14 @@
 
     def kinetic(k, streams):
         def block(n, carry):
-            rows = pl.ds(pl.multiple_of(n * 256, 256), 256)
+            rows = pl.ds(pl.multiple_of(n * 512, 512), 512)
             right = jnp.concatenate([v[s][k].reshape(16 * TILE, LANES) for s in streams], axis=1)
             part = jnp.dot(kin[rows, :], right, preferred_element_type=F32).astype(BF)
             for i, s in enumerate(streams):
-                cb[s, k, pl.ds(2 * n, 2)] = part[:, i * LANES : (i + 1) * LANES].reshape(2, TILE, LANES)
+                cb[s, k, pl.ds(4 * n, 4)] = part[:, i * LANES : (i + 1) * LANES].reshape(4, TILE, LANES)
             return carry
 
-        lax.fori_loop(0, 4, block, 0)
+        lax.fori_loop(0, 2, block, 0)
         for s in streams:
             send_parts(k, s)
 
@@ -235,11 +235,11 @@
         if k == 0:
             v[s][1, row] = applied.astype(BF)
             return
-        result = 2.0 * applied - v[s][k - 1, row].astype(F32)
         if k == 1:
-            v[s][2, row] = result.astype(BF)
+            v[s][2, row] = (2.0 * applied - v[s][0, row].astype(F32)).astype(BF)
         else:
-            out_ref[:, pl.ds(s * LANES, LANES)] = result
+            out_ref[:, pl.ds(s * LANES, LANES)] = 2.0 * applied
+            prev_ref[:, pl.ds(s * LANES, LANES)] = v[s][1, row]
 
     kept = {}
 
@@ -312,9 +312,12 @@
 def body(grid_values, external, tiles, kinetic, orbitals):
     any_spec = pl.BlockSpec(memory_space=pl.ANY)
     dma = pltpu.SemaphoreType.DMA
-    return pl.pallas_call(
+    doubled, before = pl.pallas_call(
         kernel,
-        out_shape=jax.ShapeDtypeStruct((TILE, STREAMS * LANES), F32),
+        out_shape=[
+            jax.ShapeDtypeStruct((TILE, STREAMS * LANES), F32),
+            jax.ShapeDtypeStruct((TILE, STREAMS * LANES), BF),
+        ],
         in_specs=[
             any_spec,
             any_spec,
@@ -322,7 +325,7 @@
             any_spec,
             any_spec,
         ],
-        out_specs=pl.BlockSpec(memory_space=pltpu.VMEM),
+        out_specs=[pl.BlockSpec(memory_space=pltpu.VMEM)] * 2,
         scratch_shapes=[
             pltpu.VMEM(kinetic.shape, BF),
             pltpu.VMEM((BATCH, PTS, LIST), BF),
@@ -352,9 +355,10 @@
             dma((STREAMS,)),
         ],
         compiler_params=pltpu.CompilerParams(
-            collective_id=0, has_side_effects=True, vmem_limit_bytes=60 * 1024 * 1024
+            collective_id=0, has_side_effects=True, vmem_limit_bytes=62914560
         ),
     )(tiles, external, grid_values, kinetic, orbitals)
+    return doubled - before.astype(F32)
 
 
 def solution(mesh):

time: 66 us -> 66.1 us (level)
  other arithmetic: 0 us -> 1.58 us
  local copies, waits for them, and re-layouts: 1.57 us -> 0 us
    sub x0 -> x1, other arithmetic: none -> 1.58 us  [body(): return doubled - before.astype(F32)]
    unnamed x1 -> x0, local copies, waits for them, and re-layouts: 1.57 us -> none
where the time goes in v4:
time: 66.1 us; the launch traced here: 66 us
  Pallas kernels  64.4 us (97%)
  other arithmetic  1.58 us (2%)
    pallas_call x1, Pallas kernels, body(): pl.pallas_call(kernel, out_shape=[jax.ShapeDtypeStruct((TILE, STREAMS * L...  64.4 us
    sub x1, other arithmetic, body(): return doubled - before.astype(F32)  1.58 us

profile of v4, /device:TPU:0, one launch (start us, length us, event | category | flops | bytes accessed | tf_op | source)
XLA Modules:
  0.0 66.0 jit_solution(11450924091942495046)
XLA Ops:
  0.0 64.4 %shard_map.55 = (f32[128,256]{1,0:T(8,128)}, bf16[128,256]{1,0:T(8,128)(2,1)}) custom-call(s32[4,3]{1,0:T(4,128)} %tiles_hbm.1, f32[4,256]{1,0:T(4,128)} %ext_hbm.1, bf16[4,256,384]{2,1,0:T(8,128)(2,1)} %g_hbm.1, bf16[1024,2048]{1,0:T(8,128)(2,1)} %k_hbm.1, bf16[128,256]{1,0:T(8,128)(2,1)} %orb_hbm.1), custom_call_target="tpu_custom_call" | custom-call | tf_op jit(solution)/shard_map/pallas_call | solution.py:315
  64.4 1.6 %convert_subtract_fusion = f32[128,256]{1,0:T(8,128)} fusion(f32[128,256]{1,0:T(8,128)} %get-tuple-element.7, bf16[128,256]{1,0:T(8,128)(2,1)} %get-tuple-element.8), kind=kLoop, calls=%fused_computation | loop fusion | flops 65536 | bytes 327680 | tf_op jit(solution)/shard_map/sub | solution.py:361

commit v5 on v3

--- a/solution.py
+++ b/solution.py
@@ -207,24 +207,30 @@
             send_parts(k, s)
 
     def pass_on(k, s):
-        kept = []
-        for q in (*FAR, 0):
+        for q in FAR:
             arrived(r1.at[s, k, q], r1_r.at[k, s, q])
             for h in range(2):
                 own = sb.at[s, k, tile_of(h, 0, q), pl.ds(h * HALF, HALF)]
                 total = own[...].astype(F32)
                 for n in range(3):
                     total = total + r1[s, k, q, h, n].astype(F32)
-                if q == 0:
-                    kept.append(total)
-                    continue
                 own[...] = total.astype(BF)
                 start(own, r2.at[s, k, h, 3 - q], r2_s.at[s], r2_r.at[k, s], (tile_of(h, 0, q), col))
-        return jnp.concatenate(kept, axis=0)
-
-    def collect(k, s, kept):
+
+    def keep(k, s):
+        arrived(r1.at[s, k, 0], r1_r.at[k, s, 0])
+        halves = []
+        for h in range(2):
+            total = sb[s, k, row, pl.ds(h * HALF, HALF)].astype(F32)
+            for n in range(3):
+                total = total + r1[s, k, 0, h, n].astype(F32)
+            halves.append(total)
+        return jnp.concatenate(halves, axis=0)
+
+    def collect(k, s):
+        total = keep(k, s)
         arrived(cr.at[s, k], c_r.at[k, s])
-        total = kept + cb[s, k, col].astype(F32)
+        total = total + cb[s, k, col].astype(F32)
         for n in range(7):
             total = total + cr[s, k, n].astype(F32)
         arrived(r2.at[s, k], r2_r.at[k, s])
@@ -240,8 +246,6 @@
             v[s][2, row] = result.astype(BF)
         else:
             out_ref[:, pl.ds(s * LANES, LANES)] = result
-
-    kept = {}
 
     def step(name, k, s):
         with jax.named_scope(f"{name}{k}{s}"):
@@ -259,9 +263,9 @@
             elif name == "kin":
                 kinetic(k, (0, 1) if k == 0 else (s,))
             elif name == "pass":
-                kept[k, s] = pass_on(k, s)
+                pass_on(k, s)
             elif name == "coll":
-                collect(k, s, kept[k, s])
+                collect(k, s)
 
     step("own", 0, 0)
     step("own", 0, 1)

time: 66 us -> 66 us (level)
  no operation moved by 1% of the time
where the time goes in v5:
time: 66 us; the launch traced here: 65.9 us
  Pallas kernels  64.3 us (97%)
  local copies, waits for them, and re-layouts  1.57 us (2%)
    pallas_call x1, Pallas kernels, body(): pl.pallas_call(kernel, out_shape=jax.ShapeDtypeStruct((TILE, STREAMS * LA...  64.3 us
    unnamed x1, local copies, waits for them, and re-layouts  1.57 us

profile of v5, /device:TPU:0, one launch (start us, length us, event | category | flops | bytes accessed | tf_op | source)
XLA Modules:
  0.0 65.9 jit_solution(17943043770402644816)
XLA Ops:
  0.0 64.3 %shard_map.55 = f32[128,256]{1,0:T(8,128)} custom-call(s32[4,3]{1,0:T(4,128)} %tiles_hbm.1, f32[4,256]{1,0:T(4,128)} %ext_hbm.1, bf16[4,256,384]{2,1,0:T(8,128)(2,1)} %g_hbm.1, bf16[1024,2048]{1,0:T(8,128)(2,1)} %k_hbm.1, bf16[128,256]{1,0:T(8,128)(2,1)} %orb_hbm.1), custom_call_target="tpu_custom_call" | custom-call | tf_op jit(solution)/shard_map/pallas_call | solution.py:319
  64.4 1.6 %copy.7 = f32[128,256]{1,0:T(8,128)} copy(f32[128,256]{1,0:T(8,128)} %shard_map.55) | data formatting | bytes 262144
